TPU v7x, 32 devices: a whole 2x2x4 slice. The times are simulated.
32 devices in a mesh: row: 8 (over z, x), col: 4 (over y, core).
Axes of the slice: x: 2, y: 2, z: 4, core: 2. Of those that a mesh axis runs over, the one named last changes fastest.
Arguments:
- tensor: float32 [32, 1024, 1024], P(None, 'row', 'col'), may hold values from -6 to 6
- initial_first: float32 [1024, 256], P('row'), may hold values from -6 to 6
- initial_second: float32 [1024, 256], P('col'), may hold values from -6 to 6
Outputs:
- factor_first: float32 [1024, 256], P('row')
- factor_second: float32 [1024, 256], P('col')
- factor_frames: float32 [32, 256], replicated
- weights: float32 [256], replicated
All inputs are finite; a program needn't handle non-finite values.
Results may differ from a plain program's by a relative error of at most 0.00024.
Values sent between devices are 32-bit elements; how exact they have to be, the bound alone decides.
A program may use at most 128 MiB of HBM per device.

v0:
```python
import math
import jax
import jax.numpy as jnp
from jax import lax
from jax.sharding import PartitionSpec as P

PASSES = 2
epsilon = 1e-06


def solve_gram(partials, hadamard):
    factor_lower = jnp.linalg.cholesky(hadamard)
    midway = lax.linalg.triangular_solve(
        factor_lower, partials, left_side=False, lower=True, transpose_a=True
    )
    return lax.linalg.triangular_solve(
        factor_lower, midway, left_side=False, lower=True, transpose_a=False
    )


def local_gram(matrix):
    return jnp.dot(matrix.T, matrix, precision=lax.Precision.HIGHEST)


def normalize_second(unscaled, row_count):
    squares = lax.psum(jnp.sum(unscaled * unscaled, axis=0), "col")
    scaling = jnp.sqrt(squares / row_count + epsilon)
    normed = unscaled / scaling
    gram_new = lax.psum(local_gram(normed), "col") / row_count
    return (normed, gram_new)


def body(tensor, initial_first, initial_second):
    highest = lax.Precision.HIGHEST
    frames = tensor.shape[0]
    rows_first = tensor.shape[1] * lax.axis_size("row")
    rows_second = tensor.shape[2] * lax.axis_size("col")
    first_gram = lax.psum(local_gram(initial_first), "row") / rows_first
    second = initial_second
    second_gram = lax.psum(local_gram(initial_second), "col") / rows_second
    contracted = jnp.einsum("kij,ir->kjr", tensor, initial_first, precision=highest)
    for repeat in range(PASSES):
        frame_terms = jnp.einsum("kjr,jr->kr", contracted, second, precision=highest)
        frame_sums = lax.psum(frame_terms, ("row", "col"))
        frame_raw = solve_gram(frame_sums, first_gram * second_gram) / math.sqrt(
            rows_first * rows_second
        )
        frame_scaling = jnp.sqrt(jnp.mean(frame_raw * frame_raw, axis=0) + epsilon)
        factor_frames = frame_raw / frame_scaling
        frame_gram = local_gram(factor_frames) / frames
        second_terms = jnp.einsum("kjr,kr->jr", contracted, factor_frames, precision=highest)
        hadamard = first_gram * frame_gram
        own_rows = lax.psum_scatter(second_terms, "row", scatter_dimension=0, tiled=True)
        solved_rows = solve_gram(own_rows, hadamard) / math.sqrt(rows_first * frames)
        second_raw = lax.all_gather(solved_rows, "row", axis=0, tiled=True)
        second, second_gram = normalize_second(second_raw, rows_second)
    second_contracted = jnp.einsum("kij,jr->kir", tensor, second, precision=highest)
    first_terms = jnp.einsum("kir,kr->ir", second_contracted, factor_frames, precision=highest)
    hadamard = second_gram * frame_gram
    own_rows = lax.psum_scatter(first_terms, "col", scatter_dimension=0, tiled=True)
    solved_rows = solve_gram(own_rows, hadamard) / math.sqrt(rows_second * frames)
    first_raw = lax.all_gather(solved_rows, "col", axis=0, tiled=True)
    squares = lax.psum(jnp.sum(first_raw * first_raw, axis=0), "row")
    weights = jnp.sqrt(squares / rows_first + epsilon)
    factor_first = first_raw / weights
    return (factor_first, second, factor_frames, weights)


def solution(mesh):
    placed = (P(None, "row", "col"), P("row", None), P("col", None))
    return jax.shard_map(
        body,
        mesh=mesh,
        in_specs=placed,
        out_specs=(P("row", None), P("col", None), P(), P()),
        check_vma=False,
    )
```

profile of v0, /device:TPU:0, one launch (start us, length us, event | category | flops | bytes accessed | tf_op | source)
XLA Modules:
  0.0 647.6 jit_solution(8311122888523446965)
XLA Ops:
  7.2 2.4 fusion.93
  9.7 1.1 fusion.92
  10.9 10.7 %multiply_reduce_fusion.3 = (f32[256,32]{0,1:T(8,128)S(1)}, f32[32,256,256]{2,1,0:T(8,128)}) fusion(f32[256,256]{0,1:T(8,128)} %bitcast.270, f32[32,128,256]{2,1,0:T(8,128)} %param.8, f32[128,256]{1,0:T(8,128)S(1)} %copy-done), kind=kOutput, calls=%fused_computation.13 | convolution fusion | flops 3225411584 | bytes 13008896 | tf_op jit(solution)/shard_map/kij,ir->kjr/dot_general | solution.py:41
  21.7 43.2 %psum.65 = f32[32,256]{0,1:T(8,128)S(1)} all-reduce(f32[32,256]{0,1:T(8,128)S(1)} %bitcast.276), channel_id=1, replica_groups=mesh['row'=8,'col'=4] {'row','col'}, use_global_device_ids=true, to_apply=%region_6.0 | all-reduce | flops 8192 | bytes 65536 | tf_op jit(solution)/shard_map/psum | solution.py:44
  65.0 55.4 %all-reduce.6.cloned.1.call-done = f32[256,256]{0,1:T(8,128)} async-done(((f32[256,256]{0,1:T(8,128)}), f32[256,256]{0,1:T(8,128)}) %all-reduce.6.cloned.1.call-update) | async-done | bytes 262160 | tf_op jit(solution)/shard_map/psum | solution.py:38
  120.4 1.1 multiply_multiply_fusion.2
  121.7 11.7 %cholesky.256 = f32[128,128]{1,0:T(8,128)S(1)} custom-call(f32[128,128]{1,0:T(8,128)S(1)} %cholesky.422), custom_call_target="Cholesky" | custom-call | tf_op jit(solution)/shard_map/jit(cholesky)/cholesky | solution.py:12
  133.5 9.8 %custom-call.26 = f32[1,128,128]{1,2,0:T(8,128)S(1)} custom-call(f32[1,128,128]{2,1,0:T(8,128)S(1)} %get-tuple-element.150), custom_call_target="InvertDiagBlocksLowerTriangular" | custom-call | tf_op jit(solution)/shard_map/jit(cholesky)/cholesky | solution.py:12
  143.8 11.7 %cholesky.273 = f32[128,128]{1,0:T(8,128)S(1)} custom-call(f32[128,128]{1,0:T(8,128)S(1)} %convolution_subtract_fusion.9), custom_call_target="Cholesky" | custom-call | tf_op jit(solution)/shard_map/jit(cholesky)/cholesky | solution.py:12
  157.6 4.0 while.20
  158.2 1.4 bitcast_dynamic-update-slice_fusion.10
  160.2 1.4 bitcast_dynamic-update-slice_fusion.10
  161.6 20.1 %custom-call.27 = f32[2,128,128]{1,2,0:T(8,128)S(1)} custom-call(f32[2,128,128]{2,1,0:T(8,128)S(1)} %get-tuple-element.71), custom_call_target="InvertDiagBlocksLowerTriangular" | custom-call | tf_op jit(solution)/shard_map/triangular_solve/custom-call.0 | solution.py:13
  183.1 4.9 multiply_reduce_fusion.2
  188.7 11.7 %cholesky.290 = f32[128,128]{1,0:T(8,128)S(1)} custom-call(f32[128,128]{1,0:T(8,128)S(1)} %cholesky.425), custom_call_target="Cholesky" | custom-call | tf_op jit(solution)/shard_map/jit(cholesky)/cholesky | solution.py:12
  200.5 9.8 %custom-call.29 = f32[1,128,128]{1,2,0:T(8,128)S(1)} custom-call(f32[1,128,128]{2,1,0:T(8,128)S(1)} %get-tuple-element.146), custom_call_target="InvertDiagBlocksLowerTriangular" | custom-call | tf_op jit(solution)/shard_map/jit(cholesky)/cholesky | solution.py:12
  210.8 11.7 %cholesky.307 = f32[128,128]{1,0:T(8,128)S(1)} custom-call(f32[128,128]{1,0:T(8,128)S(1)} %convolution_subtract_fusion.7), custom_call_target="Cholesky" | custom-call | tf_op jit(solution)/shard_map/jit(cholesky)/cholesky | solution.py:12
  225.1 4.2 while.21
  225.9 1.4 bitcast_dynamic-update-slice_fusion.11
  227.9 1.4 bitcast_dynamic-update-slice_fusion.11
  229.3 19.7 %custom-call.30 = f32[2,128,128]{1,2,0:T(8,128)S(1)} custom-call(f32[2,128,128]{2,1,0:T(8,128)S(1)} %get-tuple-element.73), custom_call_target="InvertDiagBlocksLowerTriangular" | custom-call | tf_op jit(solution)/shard_map/triangular_solve/custom-call.0 | solution.py:13
  249.0 0.8 reduce-scatter.10.cloned.1.call-done
  250.6 0.9 fusion.54
  252.6 30.9 %all_gather.9 = f32[256,256]{1,0:T(8,128)S(1)} all-gather(f32[32,256]{1,0:T(8,128)S(1)} %maximum_multiply_fusion.1), channel_id=1, replica_groups=mesh['row'=8,'col'=4] {'row'}, dimensions={0}, use_global_device_ids=true | all-gather | bytes 294912 | tf_op jit(solution)/shard_map/all_gather | solution.py:55
  283.5 5.7 psum.66
  289.3 1.3 fusion.14
  290.6 4.2 multiply_reduce_fusion.1
  294.9 39.1 %psum.68 = f32[32,256]{0,1:T(8,128)S(1)} all-reduce(f32[32,256]{0,1:T(8,128)S(1)} %bitcast.277), channel_id=1, replica_groups=mesh['row'=8,'col'=4] {'row','col'}, use_global_device_ids=true, to_apply=%region_12.16 | all-reduce | flops 8192 | bytes 65536 | tf_op jit(solution)/shard_map/psum | solution.py:44
  334.1 1.0 multiply_multiply_fusion.1
  335.3 11.7 %cholesky.324 = f32[128,128]{1,0:T(8,128)S(1)} custom-call(f32[128,128]{1,0:T(8,128)S(1)} %cholesky.428), custom_call_target="Cholesky" | custom-call | tf_op jit(solution)/shard_map/jit(cholesky)/cholesky | solution.py:12
  347.0 9.8 %custom-call.32 = f32[1,128,128]{1,2,0:T(8,128)S(1)} custom-call(f32[1,128,128]{2,1,0:T(8,128)S(1)} %get-tuple-element.142), custom_call_target="InvertDiagBlocksLowerTriangular" | custom-call | tf_op jit(solution)/shard_map/jit(cholesky)/cholesky | solution.py:12
  357.3 11.7 %cholesky.341 = f32[128,128]{1,0:T(8,128)S(1)} custom-call(f32[128,128]{1,0:T(8,128)S(1)} %convolution_subtract_fusion.5), custom_call_target="Cholesky" | custom-call | tf_op jit(solution)/shard_map/jit(cholesky)/cholesky | solution.py:12
  371.7 4.0 while.22
  372.3 1.4 bitcast_dynamic-update-slice_fusion.12
  374.3 1.4 bitcast_dynamic-update-slice_fusion.12
  375.7 20.1 %custom-call.33 = f32[2,128,128]{1,2,0:T(8,128)S(1)} custom-call(f32[2,128,128]{2,1,0:T(8,128)S(1)} %get-tuple-element.75), custom_call_target="InvertDiagBlocksLowerTriangular" | custom-call | tf_op jit(solution)/shard_map/triangular_solve/custom-call.0 | solution.py:13
  397.3 4.9 multiply_reduce_fusion
  402.9 11.7 %cholesky.358 = f32[128,128]{1,0:T(8,128)S(1)} custom-call(f32[128,128]{1,0:T(8,128)S(1)} %cholesky.431), custom_call_target="Cholesky" | custom-call | tf_op jit(solution)/shard_map/jit(cholesky)/cholesky | solution.py:12
  414.7 9.8 %custom-call.35 = f32[1,128,128]{1,2,0:T(8,128)S(1)} custom-call(f32[1,128,128]{2,1,0:T(8,128)S(1)} %get-tuple-element.138), custom_call_target="InvertDiagBlocksLowerTriangular" | custom-call | tf_op jit(solution)/shard_map/jit(cholesky)/cholesky | solution.py:12
  424.9 11.7 %cholesky.375 = f32[128,128]{1,0:T(8,128)S(1)} custom-call(f32[128,128]{1,0:T(8,128)S(1)} %convolution_subtract_fusion.3), custom_call_target="Cholesky" | custom-call | tf_op jit(solution)/shard_map/jit(cholesky)/cholesky | solution.py:12
  439.3 4.2 while.23
  440.1 1.4 bitcast_dynamic-update-slice_fusion.13
  442.1 1.4 bitcast_dynamic-update-slice_fusion.13
  443.5 19.7 %custom-call.36 = f32[2,128,128]{1,2,0:T(8,128)S(1)} custom-call(f32[2,128,128]{2,1,0:T(8,128)S(1)} %get-tuple-element.77), custom_call_target="InvertDiagBlocksLowerTriangular" | custom-call | tf_op jit(solution)/shard_map/triangular_solve/custom-call.0 | solution.py:13
  463.2 2.9 reduce-scatter.12.cloned.1.call-done
  466.9 0.9 fusion.61
  468.9 30.9 %all_gather.10 = f32[256,256]{1,0:T(8,128)S(1)} all-gather(f32[32,256]{1,0:T(8,128)S(1)} %maximum_multiply_fusion.3), channel_id=1, replica_groups=mesh['row'=8,'col'=4] {'row'}, dimensions={0}, use_global_device_ids=true | all-gather | bytes 294912 | tf_op jit(solution)/shard_map/all_gather | solution.py:55
  499.8 5.7 psum.69
  505.5 10.0 %fusion.4 = f32[256,32,128]{2,0,1:T(8,128)} fusion(f32[32,128,256]{2,1,0:T(8,128)} %param.8, f32[256,256]{1,0:T(8,128)S(1)} %broadcast_divide_fusion), kind=kOutput, calls=%fused_computation.40 | convolution fusion | flops 3221225472 | bytes 8650752 | tf_op jit(solution)/shard_map/kij,jr->kir/dot_general | solution.py:57
  515.5 1.3 fusion.94
  516.8 8.2 %fusion = f32[256,1,128]{2,1,0:T(1,128)S(1)} fusion(f32[32,256,1]{0,2,1:T(1,128)S(1)} %copy.67, f32[256,32,128]{2,0,1:T(8,128)} %fusion.4), kind=kOutput, calls=%fused_computation.14 | convolution fusion | flops 12582912 | bytes 4358144 | tf_op jit(solution)/shard_map/kir,kr->ir/dot_general | solution.py:58
  525.0 0.8 copy.73
  525.8 22.6 %all-reduce.12.cloned.1.call-done = f32[256,256]{0,1:T(8,128)} async-done(((f32[256,256]{0,1:T(8,128)}), f32[256,256]{0,1:T(8,128)}) %all-reduce.12.cloned.1.call-update) | async-done | bytes 262160 | tf_op jit(solution)/shard_map/psum | solution.py:29
  548.5 1.0 multiply_multiply_fusion
  549.7 11.7 %cholesky.392 = f32[128,128]{1,0:T(8,128)S(1)} custom-call(f32[128,128]{1,0:T(8,128)S(1)} %cholesky.434), custom_call_target="Cholesky" | custom-call | tf_op jit(solution)/shard_map/jit(cholesky)/cholesky | solution.py:12
  561.4 9.8 %custom-call.38 = f32[1,128,128]{1,2,0:T(8,128)S(1)} custom-call(f32[1,128,128]{2,1,0:T(8,128)S(1)} %get-tuple-element.134), custom_call_target="InvertDiagBlocksLowerTriangular" | custom-call | tf_op jit(solution)/shard_map/jit(cholesky)/cholesky | solution.py:12
  571.7 11.7 %cholesky.409 = f32[128,128]{1,0:T(8,128)S(1)} custom-call(f32[128,128]{1,0:T(8,128)S(1)} %convolution_subtract_fusion.1), custom_call_target="Cholesky" | custom-call | tf_op jit(solution)/shard_map/jit(cholesky)/cholesky | solution.py:12
  586.2 4.0 while.24
  586.8 1.4 bitcast_dynamic-update-slice_fusion.14
  588.8 1.4 bitcast_dynamic-update-slice_fusion.14
  590.2 19.9 %custom-call.39 = f32[2,128,128]{1,2,0:T(8,128)S(1)} custom-call(f32[2,128,128]{2,1,0:T(8,128)S(1)} %get-tuple-element.79), custom_call_target="InvertDiagBlocksLowerTriangular" | custom-call | tf_op jit(solution)/shard_map/triangular_solve/custom-call.0 | solution.py:13
  611.0 0.9 fusion.65
  613.0 5.4 all_gather.11
  618.4 21.4 %psum.71 = f32[256]{0:T(256)S(1)} all-reduce(f32[256]{0:T(256)S(1)} %multiply_reduce_fusion.6), channel_id=1, replica_groups=mesh['row'=8,'col'=4] {'row'}, use_global_device_ids=true, to_apply=%region_20.24 | all-reduce | flops 256 | bytes 2048 | tf_op jit(solution)/shard_map/psum | solution.py:63
  (164 shorter events, 26.6 us)
Async XLA Ops:
  7.2 2.5 copy-start
  7.2 57.8 %all-reduce.8.cloned.1.call-start = ((), (), s32[]{:S(2)}) async-start(), calls=%async_computation.4 | async-start | bytes 524288 | tf_op jit(solution)/shard_map/psum | solution.py:40
  9.6 110.8 %all-reduce.6.cloned.1.call-start = ((), (), s32[]{:S(2)}) async-start(), calls=%async_computation.3 | async-start | bytes 524288 | tf_op jit(solution)/shard_map/psum | solution.py:38
  10.8 239.0 %reduce-scatter.10.cloned.1.call-start = ((), (), s32[]{:S(2)}) async-start(), calls=%async_computation.7 | async-start | bytes 294912
  120.4 67.6 %copy-start.1 = (f32[256,256]{0,1:T(8,128)S(1)}, f32[256,256]{0,1:T(8,128)}, u32[]{:S(2)}) copy-start(f32[256,256]{0,1:T(8,128)} %all-reduce.6.cloned.1.call-done) | copy-start | bytes 786436
  188.0 146.1 %all-reduce.10.cloned.1.call-start = ((), (), s32[]{:S(2)}) async-start(), calls=%async_computation.5 | async-start | bytes 524288 | tf_op jit(solution)/shard_map/psum | solution.py:29
  290.6 175.4 %reduce-scatter.12.cloned.1.call-start = ((), (), s32[]{:S(2)}) async-start(), calls=%async_computation.8 | async-start | bytes 294912
  397.2 118.2 %copy-start.3 = (f32[32,256]{1,0:T(8,128)}, f32[32,256]{1,0:T(8,128)S(1)}, u32[]{:S(2)}) copy-start(f32[32,256]{1,0:T(8,128)S(1)} %fusion.78) | copy-start | bytes 98308
  402.2 146.3 %all-reduce.12.cloned.1.call-start = ((), (), s32[]{:S(2)}) async-start(), calls=%async_computation.6 | async-start | bytes 524288 | tf_op jit(solution)/shard_map/psum | solution.py:29
  505.5 44.2 %copy-start.2 = (f32[256,256]{1,0:T(8,128)}, f32[256,256]{1,0:T(8,128)S(1)}, u32[]{:S(2)}) copy-start(f32[256,256]{1,0:T(8,128)S(1)} %broadcast_divide_fusion) | copy-start | bytes 786436
  516.8 93.4 %reduce-scatter.14.cloned.1.call-start = ((), (), s32[]{:S(2)}) async-start(), calls=%async_computation.9 | async-start | bytes 163840
  639.8 0.7 copy-start.4
Sparse Core Ops, SparseCore 0:
  10.9 34.9 all-reduce.7
  49.3 71.0 all-reduce.5
  188.1 61.6 reduce-scatter.9
  290.7 31.6 all-reduce.9
  402.3 63.6 reduce-scatter.11
  516.9 31.5 all-reduce.11
  551.5 19.8 reduce-scatter.13
where the time goes:
time: 653 us; the launch traced here: 648 us
  other arithmetic  290 us (44%)
  blocking collectives  182 us (28%)
  waiting for transfers between devices  81.9 us (13%)
  matrix products  46.5 us (7%)
  local copies, waits for them, and re-layouts  24.2 us (4%)
  between operations  21.7 us (3%)
    another operation x34, other arithmetic, solve_gram(): factor_lower = jnp.linalg.cholesky(hadamard)  172 us
    another operation x11, other arithmetic, solve_gram(): lax.linalg.triangular_solve(factor_lower, partials, left_side=False, lowe...  99.6 us
    psum x2, blocking collectives, body(): frame_sums = lax.psum(frame_terms, ('row', 'col'))  82.3 us
    all_gather x2, blocking collectives, body(): second_raw = lax.all_gather(solved_rows, 'row', axis=0, tiled=True)  61.7 us
    psum x1, waiting for transfers between devices, body(): first_gram = lax.psum(local_gram(initial_first), 'row') / rows_first  55.4 us
    psum x2, waiting for transfers between devices, normalize_second(): gram_new = lax.psum(local_gram(normed), 'col') / row_count  22.7 us
    another operation x39, local copies, waits for them, and re-layouts, solve_gram(): lax.linalg.triangular_solve(factor_lower, partials, left_side=False, lowe...  22 us
    psum x1, blocking collectives, body(): squares = lax.psum(jnp.sum(first_raw * first_raw, axis=0), 'row')  21.4 us
  transfers between devices with their start and end apart: 7, of which 4 were waited for; matrix products, arithmetic and copies ran while one was open for 32% of the time, Pallas kernels for 0%

commit v1 on v0

--- a/solution.py
+++ b/solution.py
@@ -31,11 +31,15 @@
 
 
 def body(tensor, initial_first, initial_second):
+
+    def order_ports_for(target, axis_id):
+        return jnp.sum(jax.lax.all_gather(target, axis_id), axis=0)
+
     highest = lax.Precision.HIGHEST
     frames = tensor.shape[0]
     rows_first = tensor.shape[1] * lax.axis_size("row")
     rows_second = tensor.shape[2] * lax.axis_size("col")
-    first_gram = lax.psum(local_gram(initial_first), "row") / rows_first
+    first_gram = order_ports_for(local_gram(initial_first), "row") / rows_first
     second = initial_second
     second_gram = lax.psum(local_gram(initial_second), "col") / rows_second
     contracted = jnp.einsum("kij,ir->kjr", tensor, initial_first, precision=highest)

time: 653 us -> 674 us (1.032)
  waiting for transfers between devices: 81.9 us -> 98.1 us
    unnamed x10, waiting for transfers between devices: 3.8 us -> 75.7 us
    psum x1 -> x0, waiting for transfers between devices: 55.4 us -> none  [body(): first_gram = lax.psum(local_gram(initial_first), 'row') / rows_first]
  transfers between devices with their start and end apart: 7 -> 7, of which waited for: 4 -> 3; matrix products, arithmetic and copies ran while one was open for 32% -> 20% of each run, Pallas kernels for 0% -> 0%
where the time goes in v1:
time: 674 us; the launch traced here: 669 us
  other arithmetic  292 us (43%)
  blocking collectives  184 us (27%)
  waiting for transfers between devices  98.1 us (15%)
  matrix products  46.4 us (7%)
  local copies, waits for them, and re-layouts  25.1 us (4%)
  between operations  23 us (3%)
    another operation x34, other arithmetic, solve_gram(): factor_lower = jnp.linalg.cholesky(hadamard)  172 us
    another operation x11, other arithmetic, solve_gram(): lax.linalg.triangular_solve(factor_lower, partials, left_side=False, lowe...  99.6 us
    psum x2, blocking collectives, body(): frame_sums = lax.psum(frame_terms, ('row', 'col'))  83.7 us
    unnamed x10, waiting for transfers between devices  75.7 us
    all_gather x2, blocking collectives, body(): second_raw = lax.all_gather(solved_rows, 'row', axis=0, tiled=True)  61.8 us
    psum x2, waiting for transfers between devices, normalize_second(): gram_new = lax.psum(local_gram(normed), 'col') / row_count  22.3 us
    another operation x39, local copies, waits for them, and re-layouts, solve_gram(): lax.linalg.triangular_solve(factor_lower, partials, left_side=False, lowe...  22 us
    psum x1, blocking collectives, body(): squares = lax.psum(jnp.sum(first_raw * first_raw, axis=0), 'row')  21.4 us
  transfers between devices with their start and end apart: 7, of which 3 were waited for; matrix products, arithmetic and copies ran while one was open for 20% of the time, Pallas kernels for 0%

profile of v1, /device:TPU:0, one launch (start us, length us, event | category | flops | bytes accessed | tf_op | source)
XLA Modules:
  0.0 669.0 jit_solution(1148505227118449642)
XLA Ops:
  8.1 0.8 copy-done
  8.9 1.1 fusion.92
  10.1 2.3 fusion.93
  12.5 10.7 %multiply_reduce_fusion.3 = (f32[256,32]{0,1:T(8,128)S(1)}, f32[32,256,256]{2,1,0:T(8,128)}) fusion(f32[256,256]{0,1:T(8,128)} %bitcast.271, f32[32,128,256]{2,1,0:T(8,128)} %param.8, f32[128,256]{1,0:T(8,128)S(1)} %copy-done), kind=kOutput, calls=%fused_computation.13 | convolution fusion | flops 3225411584 | bytes 13008896 | tf_op jit(solution)/shard_map/kij,ir->kjr/dot_general | solution.py:45
  23.3 44.8 %psum.57 = f32[32,256]{0,1:T(8,128)S(1)} all-reduce(f32[32,256]{0,1:T(8,128)S(1)} %bitcast.278), channel_id=1, replica_groups=mesh['row'=8,'col'=4] {'row','col'}, use_global_device_ids=true, to_apply=%region_6.0 | all-reduce | flops 8192 | bytes 65536 | tf_op jit(solution)/shard_map/psum | solution.py:48
  68.2 1.8 reduce_sum.54
  70.1 1.0 multiply_multiply_fusion.2
  71.3 11.7 %cholesky.256 = f32[128,128]{1,0:T(8,128)S(1)} custom-call(f32[128,128]{1,0:T(8,128)S(1)} %cholesky.422), custom_call_target="Cholesky" | custom-call | tf_op jit(solution)/shard_map/jit(cholesky)/cholesky | solution.py:12
  83.1 9.8 %custom-call.26 = f32[1,128,128]{1,2,0:T(8,128)S(1)} custom-call(f32[1,128,128]{2,1,0:T(8,128)S(1)} %get-tuple-element.150), custom_call_target="InvertDiagBlocksLowerTriangular" | custom-call | tf_op jit(solution)/shard_map/jit(cholesky)/cholesky | solution.py:12
  93.4 11.7 %cholesky.273 = f32[128,128]{1,0:T(8,128)S(1)} custom-call(f32[128,128]{1,0:T(8,128)S(1)} %convolution_subtract_fusion.9), custom_call_target="Cholesky" | custom-call | tf_op jit(solution)/shard_map/jit(cholesky)/cholesky | solution.py:12
  107.2 4.0 while.20
  107.8 1.4 bitcast_dynamic-update-slice_fusion.10
  109.8 1.4 bitcast_dynamic-update-slice_fusion.10
  111.2 20.1 %custom-call.27 = f32[2,128,128]{1,2,0:T(8,128)S(1)} custom-call(f32[2,128,128]{2,1,0:T(8,128)S(1)} %get-tuple-element.71), custom_call_target="InvertDiagBlocksLowerTriangular" | custom-call | tf_op jit(solution)/shard_map/triangular_solve/custom-call.0 | solution.py:13
  133.4 11.7 %cholesky.290 = f32[128,128]{1,0:T(8,128)S(1)} custom-call(f32[128,128]{1,0:T(8,128)S(1)} %cholesky.425), custom_call_target="Cholesky" | custom-call | tf_op jit(solution)/shard_map/jit(cholesky)/cholesky | solution.py:12
  145.1 9.8 %custom-call.29 = f32[1,128,128]{1,2,0:T(8,128)S(1)} custom-call(f32[1,128,128]{2,1,0:T(8,128)S(1)} %get-tuple-element.146), custom_call_target="InvertDiagBlocksLowerTriangular" | custom-call | tf_op jit(solution)/shard_map/jit(cholesky)/cholesky | solution.py:12
  155.4 11.7 %cholesky.307 = f32[128,128]{1,0:T(8,128)S(1)} custom-call(f32[128,128]{1,0:T(8,128)S(1)} %convolution_subtract_fusion.7), custom_call_target="Cholesky" | custom-call | tf_op jit(solution)/shard_map/jit(cholesky)/cholesky | solution.py:12
  168.5 4.9 multiply_reduce_fusion.2
  174.9 4.0 while.21
  175.5 1.4 bitcast_dynamic-update-slice_fusion.11
  177.5 1.4 bitcast_dynamic-update-slice_fusion.11
  178.9 19.7 %custom-call.30 = f32[2,128,128]{1,2,0:T(8,128)S(1)} custom-call(f32[2,128,128]{2,1,0:T(8,128)S(1)} %get-tuple-element.73), custom_call_target="InvertDiagBlocksLowerTriangular" | custom-call | tf_op jit(solution)/shard_map/triangular_solve/custom-call.0 | solution.py:13
  198.6 37.3 %reduce-scatter.10.cloned.1.call-done = f32[32,256]{1,0:T(8,128)} async-done(((f32[256,256]{1,0:T(8,128)}), f32[32,256]{1,0:T(8,128)}) %reduce-scatter.10.cloned.1.call-update) | async-done | bytes 32784
  236.7 0.9 fusion.54
  238.7 30.9 %all_gather.17 = f32[256,256]{1,0:T(8,128)S(1)} all-gather(f32[32,256]{1,0:T(8,128)S(1)} %maximum_multiply_fusion.1), channel_id=1, replica_groups=mesh['row'=8,'col'=4] {'row'}, dimensions={0}, use_global_device_ids=true | all-gather | bytes 294912 | tf_op jit(solution)/shard_map/all_gather | solution.py:59
  269.7 5.7 psum.58
  275.3 1.3 fusion.14
  276.8 4.2 multiply_reduce_fusion.1
  281.1 38.9 %psum.60 = f32[32,256]{0,1:T(8,128)S(1)} all-reduce(f32[32,256]{0,1:T(8,128)S(1)} %bitcast.279), channel_id=1, replica_groups=mesh['row'=8,'col'=4] {'row','col'}, use_global_device_ids=true, to_apply=%region_12.16 | all-reduce | flops 8192 | bytes 65536 | tf_op jit(solution)/shard_map/psum | solution.py:48
  320.0 1.0 multiply_multiply_fusion.1
  321.2 11.7 %cholesky.324 = f32[128,128]{1,0:T(8,128)S(1)} custom-call(f32[128,128]{1,0:T(8,128)S(1)} %cholesky.428), custom_call_target="Cholesky" | custom-call | tf_op jit(solution)/shard_map/jit(cholesky)/cholesky | solution.py:12
  333.0 9.8 %custom-call.32 = f32[1,128,128]{1,2,0:T(8,128)S(1)} custom-call(f32[1,128,128]{2,1,0:T(8,128)S(1)} %get-tuple-element.142), custom_call_target="InvertDiagBlocksLowerTriangular" | custom-call | tf_op jit(solution)/shard_map/jit(cholesky)/cholesky | solution.py:12
  343.3 11.7 %cholesky.341 = f32[128,128]{1,0:T(8,128)S(1)} custom-call(f32[128,128]{1,0:T(8,128)S(1)} %convolution_subtract_fusion.5), custom_call_target="Cholesky" | custom-call | tf_op jit(solution)/shard_map/jit(cholesky)/cholesky | solution.py:12
  357.7 4.0 while.22
  358.3 1.4 bitcast_dynamic-update-slice_fusion.12
  360.3 1.4 bitcast_dynamic-update-slice_fusion.12
  361.7 20.1 %custom-call.33 = f32[2,128,128]{1,2,0:T(8,128)S(1)} custom-call(f32[2,128,128]{2,1,0:T(8,128)S(1)} %get-tuple-element.75), custom_call_target="InvertDiagBlocksLowerTriangular" | custom-call | tf_op jit(solution)/shard_map/triangular_solve/custom-call.0 | solution.py:13
  383.8 11.7 %cholesky.358 = f32[128,128]{1,0:T(8,128)S(1)} custom-call(f32[128,128]{1,0:T(8,128)S(1)} %cholesky.431), custom_call_target="Cholesky" | custom-call | tf_op jit(solution)/shard_map/jit(cholesky)/cholesky | solution.py:12
  395.6 9.8 %custom-call.35 = f32[1,128,128]{1,2,0:T(8,128)S(1)} custom-call(f32[1,128,128]{2,1,0:T(8,128)S(1)} %get-tuple-element.138), custom_call_target="InvertDiagBlocksLowerTriangular" | custom-call | tf_op jit(solution)/shard_map/jit(cholesky)/cholesky | solution.py:12
  405.9 11.7 %cholesky.375 = f32[128,128]{1,0:T(8,128)S(1)} custom-call(f32[128,128]{1,0:T(8,128)S(1)} %convolution_subtract_fusion.3), custom_call_target="Cholesky" | custom-call | tf_op jit(solution)/shard_map/jit(cholesky)/cholesky | solution.py:12
  418.9 4.9 multiply_reduce_fusion
  425.2 4.0 while.23
  425.9 1.4 bitcast_dynamic-update-slice_fusion.13
  427.8 1.4 bitcast_dynamic-update-slice_fusion.13
  429.2 19.7 %custom-call.36 = f32[2,128,128]{1,2,0:T(8,128)S(1)} custom-call(f32[2,128,128]{2,1,0:T(8,128)S(1)} %get-tuple-element.77), custom_call_target="InvertDiagBlocksLowerTriangular" | custom-call | tf_op jit(solution)/shard_map/triangular_solve/custom-call.0 | solution.py:13
  449.0 38.3 %reduce-scatter.12.cloned.1.call-done = f32[32,256]{1,0:T(8,128)} async-done(((f32[256,256]{1,0:T(8,128)}), f32[32,256]{1,0:T(8,128)}) %reduce-scatter.12.cloned.1.call-update) | async-done | bytes 32784
  488.2 0.9 fusion.61
  490.2 30.9 %all_gather.18 = f32[256,256]{1,0:T(8,128)S(1)} all-gather(f32[32,256]{1,0:T(8,128)S(1)} %maximum_multiply_fusion.3), channel_id=1, replica_groups=mesh['row'=8,'col'=4] {'row'}, dimensions={0}, use_global_device_ids=true | all-gather | bytes 294912 | tf_op jit(solution)/shard_map/all_gather | solution.py:59
  521.1 5.7 psum.61
  526.9 1.3 fusion.94
  528.2 9.8 %fusion.4 = f32[256,32,128]{2,0,1:T(8,128)} fusion(f32[32,128,256]{2,1,0:T(8,128)} %param.8, f32[256,256]{1,0:T(8,128)S(1)} %broadcast_divide_fusion), kind=kOutput, calls=%fused_computation.40 | convolution fusion | flops 3221225472 | bytes 8650752 | tf_op jit(solution)/shard_map/kij,jr->kir/dot_general | solution.py:61
  538.1 8.2 %fusion = f32[256,1,128]{2,1,0:T(1,128)S(1)} fusion(f32[32,256,1]{0,2,1:T(1,128)S(1)} %copy.65, f32[256,32,128]{2,0,1:T(8,128)} %fusion.4), kind=kOutput, calls=%fused_computation.14 | convolution fusion | flops 12582912 | bytes 4358144 | tf_op jit(solution)/shard_map/kir,kr->ir/dot_general | solution.py:62
  547.1 22.3 %all-reduce.9.cloned.1.call-done = f32[256,256]{0,1:T(8,128)} async-done(((f32[256,256]{0,1:T(8,128)}), f32[256,256]{0,1:T(8,128)}) %all-reduce.9.cloned.1.call-update) | async-done | bytes 262160 | tf_op jit(solution)/shard_map/psum | solution.py:29
  569.4 1.0 multiply_multiply_fusion
  570.6 11.7 %cholesky.392 = f32[128,128]{1,0:T(8,128)S(1)} custom-call(f32[128,128]{1,0:T(8,128)S(1)} %cholesky.434), custom_call_target="Cholesky" | custom-call | tf_op jit(solution)/shard_map/jit(cholesky)/cholesky | solution.py:12
  582.3 9.8 %custom-call.38 = f32[1,128,128]{1,2,0:T(8,128)S(1)} custom-call(f32[1,128,128]{2,1,0:T(8,128)S(1)} %get-tuple-element.134), custom_call_target="InvertDiagBlocksLowerTriangular" | custom-call | tf_op jit(solution)/shard_map/jit(cholesky)/cholesky | solution.py:12
  592.6 11.7 %cholesky.409 = f32[128,128]{1,0:T(8,128)S(1)} custom-call(f32[128,128]{1,0:T(8,128)S(1)} %convolution_subtract_fusion.1), custom_call_target="Cholesky" | custom-call | tf_op jit(solution)/shard_map/jit(cholesky)/cholesky | solution.py:12
  607.1 4.0 while.24
  607.7 1.4 bitcast_dynamic-update-slice_fusion.14
  609.7 1.4 bitcast_dynamic-update-slice_fusion.14
  611.1 19.9 %custom-call.39 = f32[2,128,128]{1,2,0:T(8,128)S(1)} custom-call(f32[2,128,128]{2,1,0:T(8,128)S(1)} %get-tuple-element.79), custom_call_target="InvertDiagBlocksLowerTriangular" | custom-call | tf_op jit(solution)/shard_map/triangular_solve/custom-call.0 | solution.py:13
  631.9 0.9 fusion.65
  633.9 5.4 all_gather.19
  639.3 21.4 %psum.63 = f32[256]{0:T(256)S(1)} all-reduce(f32[256]{0:T(256)S(1)} %multiply_reduce_fusion.6), channel_id=1, replica_groups=mesh['row'=8,'col'=4] {'row'}, use_global_device_ids=true, to_apply=%region_20.24 | all-reduce | flops 256 | bytes 2048 | tf_op jit(solution)/shard_map/psum | solution.py:67
  (164 shorter events, 27.9 us)
Async XLA Ops:
  8.0 0.9 copy-start
  8.0 60.2 %all-gather.3.cloned.1.call-start = ((), (), s32[]{:S(2)}) async-start(), calls=%async_computation.6 | async-start | bytes 2359296 | tf_op jit(solution)/shard_map/all_gather | solution.py:36
  10.1 60.1 %all-reduce.5.cloned.1.call-start = ((), (), s32[]{:S(2)}) async-start(), calls=%async_computation.3 | async-start | bytes 524288 | tf_op jit(solution)/shard_map/psum | solution.py:44
  12.5 223.4 %reduce-scatter.10.cloned.1.call-start = ((), (), s32[]{:S(2)}) async-start(), calls=%async_computation.7 | async-start | bytes 294912
  173.3 146.7 %all-reduce.7.cloned.1.call-start = ((), (), s32[]{:S(2)}) async-start(), calls=%async_computation.4 | async-start | bytes 524288 | tf_op jit(solution)/shard_map/psum | solution.py:29
  276.7 210.6 %reduce-scatter.12.cloned.1.call-start = ((), (), s32[]{:S(2)}) async-start(), calls=%async_computation.8 | async-start | bytes 294912
  383.2 65.7 %copy-start.2 = (f32[32,256]{1,0:T(8,128)}, f32[32,256]{1,0:T(8,128)S(1)}, u32[]{:S(2)}) copy-start(f32[32,256]{1,0:T(8,128)S(1)} %fusion.78) | copy-start | bytes 98308
  423.8 145.6 %all-reduce.9.cloned.1.call-start = ((), (), s32[]{:S(2)}) async-start(), calls=%async_computation.5 | async-start | bytes 524288 | tf_op jit(solution)/shard_map/psum | solution.py:29
  526.9 11.2 %copy-start.1 = (f32[256,256]{1,0:T(8,128)}, f32[256,256]{1,0:T(8,128)S(1)}, u32[]{:S(2)}) copy-start(f32[256,256]{1,0:T(8,128)S(1)} %broadcast_divide_fusion) | copy-start | bytes 786436
  538.0 93.0 %reduce-scatter.14.cloned.1.call-start = ((), (), s32[]{:S(2)}) async-start(), calls=%async_computation.9 | async-start | bytes 163840
  660.7 0.7 copy-start.3
Sparse Core Ops, SparseCore 0:
  10.9 51.8 all-gather.2
  173.5 62.3 reduce-scatter.9
  423.9 63.4 reduce-scatter.11
Sparse Core Ops, SparseCore 1:
  13.4 34.8 all-reduce.4
  276.8 31.2 all-reduce.6
  538.1 31.2 all-reduce.8
  572.4 19.8 reduce-scatter.13
